TPU v7x, 32 devices: a whole 2x2x4 slice. The times are simulated.
32 devices in a mesh: intra: 4 (over y, x), inter: 8 (over z, core).
Axes of the slice: x: 2, y: 2, z: 4, core: 2. Of those that a mesh axis runs over, the one named last changes fastest.
Arguments:
- acts: bfloat16 [4096, 4096], P(('intra', 'inter')), may hold values from -6 to 6
- grad_out: bfloat16 [4096, 512], P(('intra', 'inter')), may hold values from -6 to 6
- codes: int32 [4096, 512], P('intra'), may hold values from -127 to 127
- scales: float32 [2048], P('intra'), may hold values from 0.0002 to 0.0008
Outputs:
- grad_in: bfloat16 [4096, 4096], P(('intra', 'inter'))
- grad_w: float32 [4096, 512], P(('intra', 'inter'))
All inputs are finite; a program needn't handle non-finite values.
Results may differ from a plain program's by a relative error of at most 0.0049.
Values may be sent and summed in bfloat16 or wider, within the bound.
A program may use at most 64 MiB of HBM per device.

v0:
```python
import math

import jax
import jax.numpy as jnp
from jax import lax
from jax.sharding import PartitionSpec as P


def per_device(acts, grad_out, codes, scales):
    rows = codes.shape[0]
    width_kv = codes.shape[1]
    blocks = codes.astype(jnp.float32).reshape(rows // 2, 2 * width_kv) * scales[:, None]
    local_weight = blocks.reshape(rows, width_kv).astype(jnp.bfloat16)
    n_group = lax.axis_size("intra")
    n_cross = lax.axis_size("inter")
    tok_rows = acts.shape[0]
    factor = 1.0 / math.sqrt(tok_rows * n_group * n_cross)
    contract = (((0,), (0,)), ((), ()))
    group_cot = lax.all_gather(grad_out, "intra", axis=0, tiled=True)
    columns_owned = lax.all_to_all(acts, "intra", split_axis=1, concat_axis=0, tiled=True)
    grad_w = lax.psum_scatter(
        lax.dot_general(columns_owned, group_cot, contract, preferred_element_type=jnp.float32)
        * factor,
        "inter",
        scatter_dimension=0,
        tiled=True,
    )
    pieces = jnp.dot(group_cot, local_weight.T, preferred_element_type=jnp.float32).astype(
        jnp.bfloat16
    )
    grad_in = lax.all_to_all(pieces, "intra", split_axis=0, concat_axis=1, tiled=True)
    return (grad_in, grad_w)


def solution(mesh):
    in_specs = (
        P(("intra", "inter"), None),
        P(("intra", "inter"), None),
        P("intra", None),
        P("intra"),
    )
    out_specs = (P(("intra", "inter"), None), P(("intra", "inter"), None))
    return jax.shard_map(
        per_device, mesh=mesh, in_specs=in_specs, out_specs=out_specs, check_vma=False
    )
```

profile of v0, /device:TPU:0, one launch (start us, length us, event | category | flops | bytes accessed | tf_op | source)
XLA Modules:
  0.0 80.3 jit_solution(17842315218123064964)
XLA Ops:
  7.2 0.0 copy-start.1
  7.2 2.3 %copy.9 = bf16[128,4096]{0,1:T(8,128)(2,1)} copy(bf16[128,4096]{1,0:T(8,128)(2,1)} %param.4) | data formatting | bytes 2097152 | tf_op args[0]
  9.5 5.2 %all-to-all-start.1 = ((bf16[128,4,1024]{0,2,1:T(8,128)(2,1)}), bf16[128,4,1024]{0,2,1:T(8,128)(2,1)S(1)}, u32[]{:S(2)}, u32[]{:S(2)}) async-start(bf16[128,4,1024]{0,2,1:T(8,128)(2,1)} %bitcast.3), calls=%async_computation.1 | async-start | bytes 2097152 | tf_op jit(solution)/shard_map/all_to_all | solution.py:20
  14.7 0.0 reduce-scatter.2.cloned.1.call-start
  14.7 0.0 copy-done.1
  14.7 19.4 %all_gather.3 = bf16[512,512]{1,0:T(8,128)(2,1)S(1)} all-gather(bf16[128,512]{1,0:T(8,128)(2,1)S(1)} %copy-done.1), channel_id=1, replica_groups=mesh['intra'=4,'inter'=8] {'intra'}, dimensions={0}, use_global_device_ids=true | all-gather | bytes 655360 | tf_op jit(solution)/shard_map/all_gather | solution.py:19
  34.1 0.0 all-to-all-done.1
  34.1 0.5 copy.10
  34.7 0.0 copy-start.2
  34.7 2.1 %convolution_multiply_fusion = f32[1024,512]{1,0:T(8,128)} fusion(bf16[512,1024]{1,0:T(8,128)(2,1)S(1)} %bitcast.12, bf16[512,512]{1,0:T(8,128)(2,1)S(1)} %all_gather.3), kind=kOutput, calls=%fused_computation.1 | convolution fusion | flops 537395200 | bytes 3670016 | tf_op jit(solution)/shard_map/dot_general | solution.py:22
  36.8 0.0 copy-start
  36.8 0.0 reduce-scatter.2.cloned.1.call-update
  36.8 0.0 copy-done.2
  36.8 0.1 mul.19
  36.9 0.2 mul.20
  37.1 1.3 %copy-done = s32[1024,512]{1,0:T(8,128)S(1)} copy-done((s32[1024,512]{1,0:T(8,128)S(1)}, s32[1024,512]{1,0:T(8,128)}, u32[]{:S(2)}) %copy-start) | copy-done | bytes 2097176
  38.4 0.8 %convolution_convert_fusion = bf16[1024,512]{0,1:T(8,128)(2,1)S(1)} fusion(bf16[512,512]{1,0:T(8,128)(2,1)S(1)} %all_gather.3, s32[1024,512]{1,0:T(8,128)S(1)} %copy-done, f32[1024]{0:T(1024)S(1)} %mul.20), kind=kOutput, calls=%fused_computation.2 | convolution fusion | flops 538968064 | bytes 3674112 | tf_op jit(solution)/shard_map/dot_general | solution.py:28
  39.2 14.9 %all_to_all.38 = bf16[4,128,1024]{2,1,0:T(8,128)(2,1)S(1)} all-to-all(bf16[4,128,1024]{2,1,0:T(8,128)(2,1)S(1)} %bitcast.15), channel_id=1, replica_groups=mesh['intra'=4,'inter'=8] {'intra'}, dimensions={0} | all-to-all | bytes 2097152 | tf_op jit(solution)/shard_map/all_to_all | solution.py:31
  54.1 1.1 %copy.11 = bf16[4,16,8,1024]{3,2,0,1:T(8,128)(2,1)} copy(bf16[4,16,8,1024]{3,2,1,0:T(8,128)(2,1)S(1)} %bitcast.14) | data formatting | bytes 2097152 | tf_op jit(solution)/shard_map/all_to_all | solution.py:31
  55.1 18.4 %reduce-scatter.2.cloned.1.call-done = f32[128,512]{1,0:T(8,128)} async-done(((f32[1024,512]{1,0:T(8,128)}), f32[128,512]{1,0:T(8,128)}) %reduce-scatter.2.cloned.1.call-update) | async-done | bytes 262160 | tf_op jit(solution)/shard_map/reduce_scatter | solution.py:21
Async XLA Ops:
  7.2 7.5 %copy-start.1 = (bf16[128,512]{1,0:T(8,128)(2,1)S(1)}, bf16[128,512]{1,0:T(8,128)(2,1)}, u32[]{:S(2)}) copy-start(bf16[128,512]{1,0:T(8,128)(2,1)} %param.5) | copy-start | bytes 393220
  9.5 24.6 %all-to-all-start.1 = ((bf16[128,4,1024]{0,2,1:T(8,128)(2,1)}), bf16[128,4,1024]{0,2,1:T(8,128)(2,1)S(1)}, u32[]{:S(2)}, u32[]{:S(2)}) async-start(bf16[128,4,1024]{0,2,1:T(8,128)(2,1)} %bitcast.3), calls=%async_computation.1 | async-start | bytes 2097152 | tf_op jit(solution)/shard_map/all_to_all | solution.py:20
  14.7 58.8 %reduce-scatter.2.cloned.1.call-start = ((), (), s32[]{:S(2)}) async-start(), calls=%async_computation.3 | async-start | bytes 2359296 | tf_op jit(solution)/shard_map/reduce_scatter | solution.py:21
  34.7 2.1 %copy-start.2 = (f32[512]{0:T(512)S(1)}, f32[512]{0:T(512)}, u32[]{:S(2)}) copy-start(f32[512]{0:T(512)} %param.7) | copy-start | bytes 6148
  36.8 1.6 %copy-start = (s32[1024,512]{1,0:T(8,128)S(1)}, s32[1024,512]{1,0:T(8,128)}, u32[]{:S(2)}) copy-start(s32[1024,512]{1,0:T(8,128)} %param.6) | copy-start | bytes 6291460
Sparse Core Ops, SparseCore 0:
  36.9 36.5 reduce-scatter.1
where the time goes:
time: 80.6 us; the launch traced here: 80.3 us
  blocking collectives  34.3 us (43%)
  waiting for transfers between devices  18.4 us (23%)
  between operations  14.1 us (17%)
  local copies, waits for them, and re-layouts  5.45 us (7%)
  starting transfers between devices  5.19 us (6%)
  matrix products  2.93 us (4%)
    all_gather x1, blocking collectives, per_device(): group_cot = lax.all_gather(grad_out, 'intra', axis=0, tiled=True)  19.4 us
    reduce_scatter x1, waiting for transfers between devices, per_device(): lax.psum_scatter(lax.dot_general(columns_owned, group_cot, contract, pref...  18.4 us
    all_to_all x1, blocking collectives, per_device(): lax.all_to_all(pieces, 'intra', split_axis=0, concat_axis=1, tiled=True)  14.9 us
    all_to_all x1, starting transfers between devices, per_device(): lax.all_to_all(acts, 'intra', split_axis=1, concat_axis=0, tiled=True)  5.19 us
    unnamed x7, local copies, waits for them, and re-layouts  3.56 us
    dot_general x1, matrix products, per_device(): lax.dot_general(columns_owned, group_cot, contract, preferred_element_typ...  2.09 us
  transfers between devices with their start and end apart: 2, of which 1 were waited for; matrix products, arithmetic and copies ran while one was open for 3% of the time, Pallas kernels for 0%

commit v1 on v0

--- a/solution.py
+++ b/solution.py
@@ -1,20 +1,240 @@
+import functools
 import math
 
 import jax
 import jax.numpy as jnp
 from jax import lax
+from jax.experimental import pallas as pl
+from jax.experimental.pallas import tpu as pltpu
 from jax.sharding import PartitionSpec as P
 
-
-def per_device(acts, grad_out, codes, scales):
+MESH = pl.DeviceIdType.MESH
+
+
+def flip(index, mask, extent):
+    out = 0
+    bit = 1
+    while bit < extent:
+        digit = lax.rem(index // bit, 2)
+        out = out + bit * (1 - digit if mask & bit else digit)
+        bit *= 2
+    return out
+
+
+def kernel(
+    ni, nj, acts, go, codes, scales, gin, gw,
+    go_all, acts_v, codes_v, scale_v, code_b, ac, pieces, part, rs,
+    load_sem, go_send, go_recv, fw_send, a_send, a_recv, p_send, p_recv, r_send, r_recv,
+):
+    tok, width = acts.shape
+    kv = go.shape[1]
+    rows = codes.shape[0]
+    half = rows // 2
+    nz = nj // 2
+    blk = rows // nj
+    i = lax.axis_index("intra")
+    j = lax.axis_index("inter")
+    z = j // 2
+    c = lax.rem(j, 2)
+    oc = 1 - c
+    me = 2 * i + c
+    far = sorted(range(1, ni), key=lambda d: -bin(d).count("1"))
+    near = far[::-1]
+    peers = {d: flip(i, d, ni) for d in range(ni)}
+    cores = (c, oc)
+
+    def dev(ii, zz, cc):
+        return {"intra": ii, "inter": 2 * zz + cc}
+
+    def rdma(src, dst, s, r, where):
+        return pltpu.make_async_remote_copy(
+            src_ref=src, dst_ref=dst, send_sem=s, recv_sem=r, device_id=where, device_id_type=MESH
+        )
+
+    def go_slot(m):
+        return go_all.at[pl.ds(pl.multiple_of(m * tok, tok), tok)]
+
+    half_start = pl.multiple_of(c * half, half)
+    load_go = pltpu.make_async_copy(go, go_slot(me), load_sem.at[0])
+    load_go.start()
+    load_acts = pltpu.make_async_copy(acts, acts_v, load_sem.at[1])
+    load_acts.start()
+    load_codes = pltpu.make_async_copy(codes.at[pl.ds(half_start, half)], codes_v, load_sem.at[2])
+    load_codes.start()
+    sc_start = pl.multiple_of(c * (half // 2), half // 2)
+    load_scale = pltpu.make_async_copy(scales.at[:, pl.ds(sc_start, half // 2)], scale_v, load_sem.at[3])
+    load_scale.start()
+
+    barrier = pltpu.get_barrier_semaphore()
+    count = 0
+    for d in range(ni):
+        for k, cc in enumerate(cores):
+            if d or k:
+                pl.semaphore_signal(barrier, inc=1, device_id=dev(peers[d], z, cc), device_id_type=MESH)
+                count += 1
+    for k in range(1, nz):
+        pl.semaphore_signal(barrier, inc=1, device_id=dev(i, lax.rem(z + k, nz), c), device_id_type=MESH)
+        count += 1
+    pl.semaphore_wait(barrier, count)
+
+    sends = []
+
+    load_go.wait()
+    for d in far + [0]:
+        cc = c if d else oc
+        cp = rdma(go_slot(me), go_slot(me), go_send.at[d], go_recv.at[me], dev(peers[d], z, cc))
+        cp.start()
+        sends.append(cp)
+
+    load_acts.wait()
+    order = [lax.rem(z + k, nz) for k in range(1, nz)] + [z]
+
+    def ac_slot(h, m):
+        return ac.at[h, pl.ds(pl.multiple_of(m * tok, tok), tok)]
+
+    own = []
+    for h in order:
+        for d in far + [0]:
+            for k, cc in enumerate(cores):
+                ii = peers[d]
+                col = pl.multiple_of(ii * rows + (2 * h + cc) * blk, blk)
+                src = acts_v.at[:, pl.ds(col, blk)]
+                if d or k:
+                    m = 2 * ii + cc
+                    cp = rdma(src, ac_slot(h, me), a_send.at[m, h], a_recv.at[me, h], dev(ii, z, cc))
+                    sends.append(cp)
+                else:
+                    cp = pltpu.make_async_copy(src, ac_slot(h, me), a_recv.at[me, h])
+                    own.append(cp)
+                cp.start()
+
+    load_codes.wait()
+    code_b[...] = codes_v[...].astype(jnp.float32).astype(jnp.bfloat16)
+    load_scale.wait()
+    pick = (
+        lax.broadcasted_iota(jnp.int32, (half // 2, half), 1) // 2
+        == lax.broadcasted_iota(jnp.int32, (half // 2, half), 0)
+    ).astype(jnp.float32).astype(jnp.bfloat16)
+    rest = jnp.broadcast_to(scale_v[...], (16, half // 2))
+    row_scale = jnp.zeros((16, half), jnp.float32)
+    for _ in range(3):
+        top = rest.astype(jnp.bfloat16)
+        row_scale = row_scale + jnp.dot(top, pick, preferred_element_type=jnp.float32)
+        rest = rest - top.astype(jnp.float32)
+    row_scale = row_scale[0:1]
+
+    def wait_go(m):
+        rdma(go_slot(m), go_slot(m), go_send.at[0], go_recv.at[m], dev(i, z, oc)).wait_recv()
+
+    for d in near:
+        m = 2 * peers[d] + c
+        wait_go(m)
+        cp = rdma(go_slot(m), go_slot(m), fw_send.at[d], go_recv.at[m], dev(i, z, oc))
+        cp.start()
+        sends.append(cp)
+
+    my_cols = pl.ds(pl.multiple_of(i * rows + c * half, half), half)
+    for d in near + [0]:
+        ii = peers[d]
+        wait_go(2 * ii + oc)
+        pair = go_all[pl.ds(pl.multiple_of(2 * ii * tok, 2 * tok), 2 * tok)]
+        out = lax.dot_general(
+            pair, code_b[...], (((1,), (1,)), ((), ())), preferred_element_type=jnp.float32
+        )
+        pieces[ii] = (out * row_scale).astype(jnp.bfloat16)
+        for k, cc in enumerate(cores):
+            m = 2 * ii + cc
+            src = pieces.at[ii, pl.ds(pl.multiple_of(cc * tok, tok), tok)]
+            if d or k:
+                cp = rdma(src, gin.at[:, my_cols], p_send.at[m], p_recv.at[me], dev(ii, z, cc))
+                sends.append(cp)
+            else:
+                cp = pltpu.make_async_copy(src, gin.at[:, my_cols], p_recv.at[me])
+                own_piece = cp
+            cp.start()
+
+    cot = go_all
+    mine = None
+    for n, h in enumerate(order):
+        own[n].wait()
+        for d in range(ni):
+            for k, cc in enumerate(cores):
+                if d or k:
+                    m = 2 * peers[d] + cc
+                    rdma(ac_slot(h, m), ac_slot(h, m), a_send.at[m, h], a_recv.at[m, h], dev(i, z, oc)).wait_recv()
+        term = lax.dot_general(
+            ac[h], cot[...], (((0,), (0,)), ((), ())), preferred_element_type=jnp.float32
+        )
+        if n < nz - 1:
+            part[n] = term.astype(jnp.bfloat16)
+            cp = rdma(part.at[n], rs.at[z], r_send.at[n], r_recv.at[z], dev(i, h, c))
+            cp.start()
+            sends.append(cp)
+        else:
+            mine = term
+    for k in range(1, nz):
+        h = lax.rem(z + k, nz)
+        rdma(rs.at[h], rs.at[h], r_send.at[0], r_recv.at[h], dev(i, h, c)).wait_recv()
+        mine = mine + rs[h].astype(jnp.float32)
+    gw[...] = mine * (1.0 / math.sqrt(tok * ni * nj))
+
+    own_piece.wait()
+    for d in range(ni):
+        for k, cc in enumerate(cores):
+            if d or k:
+                ii = peers[d]
+                m = 2 * ii + cc
+                cols = pl.ds(pl.multiple_of(ii * rows + cc * half, half), half)
+                rdma(gin.at[:, cols], gin.at[:, cols], p_send.at[m], p_recv.at[m], dev(i, z, oc)).wait_recv()
+    for cp in sends:
+        cp.wait_send()
+
+
+def fused(ni, nj, acts, grad_out, codes, scales):
+    tok, width = acts.shape
+    kv = grad_out.shape[1]
+    rows = codes.shape[0]
+    half, nz, blk = rows // 2, nj // 2, rows // nj
+    group = 2 * ni
+    dma = pltpu.SemaphoreType.DMA
+    bf16 = jnp.bfloat16
+    anyspace = pl.BlockSpec(memory_space=pl.ANY)
+    return tuple(pl.pallas_call(
+        functools.partial(kernel, ni, nj),
+        out_shape=(
+            jax.ShapeDtypeStruct((tok, width), bf16),
+            jax.ShapeDtypeStruct((blk, kv), jnp.float32),
+        ),
+        in_specs=[anyspace] * 4,
+        out_specs=(anyspace, pl.BlockSpec(memory_space=pltpu.VMEM)),
+        scratch_shapes=[
+            pltpu.VMEM((group * tok, kv), bf16),
+            pltpu.VMEM((tok, width), bf16),
+            pltpu.VMEM((half, kv), jnp.int32),
+            pltpu.VMEM((1, half // 2), jnp.float32),
+            pltpu.VMEM((half, kv), bf16),
+            pltpu.VMEM((nz, group * tok, blk), bf16),
+            pltpu.VMEM((ni, 2 * tok, half), bf16),
+            pltpu.VMEM((max(nz - 1, 1), blk, kv), bf16),
+            pltpu.VMEM((nz, blk, kv), bf16),
+            dma((4,)),
+            dma((ni,)), dma((group,)), dma((ni,)),
+            dma((group, nz)), dma((group, nz)),
+            dma((group,)), dma((group,)),
+            dma((nz,)), dma((nz,)),
+        ],
+        compiler_params=pltpu.CompilerParams(collective_id=0, has_side_effects=True),
+    )(acts, grad_out, codes, scales.reshape(1, -1)))
+
+
+def plain(acts, grad_out, codes, scales):
     rows = codes.shape[0]
     width_kv = codes.shape[1]
     blocks = codes.astype(jnp.float32).reshape(rows // 2, 2 * width_kv) * scales[:, None]
     local_weight = blocks.reshape(rows, width_kv).astype(jnp.bfloat16)
     n_group = lax.axis_size("intra")
     n_cross = lax.axis_size("inter")
-    tok_rows = acts.shape[0]
-    factor = 1.0 / math.sqrt(tok_rows * n_group * n_cross)
+    factor = 1.0 / math.sqrt(acts.shape[0] * n_group * n_cross)
     contract = (((0,), (0,)), ((), ()))
     group_cot = lax.all_gather(grad_out, "intra", axis=0, tiled=True)
     columns_owned = lax.all_to_all(acts, "intra", split_axis=1, concat_axis=0, tiled=True)
@@ -33,6 +253,15 @@
 
 
 def solution(mesh):
+    ni, nj = mesh.shape["intra"], mesh.shape["inter"]
+
+    def per_device(acts, grad_out, codes, scales):
+        rows = codes.shape[0]
+        aligned = rows % (nj * 128) == 0 and rows % 512 == 0 and acts.shape[0] % 16 == 0
+        if aligned and nj % 2 == 0 and ni & (ni - 1) == 0 and acts.shape[1] == ni * rows:
+            return fused(ni, nj, acts, grad_out, codes, scales)
+        return plain(acts, grad_out, codes, scales)
+
     in_specs = (
         P(("intra", "inter"), None),
         P(("intra", "inter"), None),

time: 80.6 us -> 41.2 us (0.51)
  the two profiles are of different devices: /device:TPU:0 before, /device:TPU:1 now
where the time goes in v1:
time: 41.2 us; the launch traced here: 41 us
  Pallas kernels  37.4 us (91%)
  local copies, waits for them, and re-layouts  3.04 us (7%)
  between operations  0.65 us (2%)
    pallas_call x1, Pallas kernels, fused(): pl.pallas_call(functools.partial(kernel, ni, nj), out_shape=(jax.ShapeDty...  37.4 us
    unnamed x4, local copies, waits for them, and re-layouts  3.04 us

profile of v1, /device:TPU:1, one launch (start us, length us, event | category | flops | bytes accessed | tf_op | source)
XLA Modules:
  0.0 41.0 jit_solution(12927880230533565504)
XLA Ops:
  0.6 37.4 %shard_map.59 = (bf16[128,4096]{1,0:T(8,128)(2,1)}, f32[128,512]{1,0:T(8,128)}) custom-call(bf16[128,4096]{1,0:T(8,128)(2,1)} %acts.1, bf16[128,512]{1,0:T(8,128)(2,1)} %go.1, s32[1024,512]{1,0:T(8,128)} %codes.1, f32[1,512]{1,0:T(1,128)} %bitcast.1), custom_call_target="tpu_custom_call" | custom-call | tf_op jit(solution)/shard_map/pallas_call | solution.py:202
  38.0 0.0 copy-start
  38.0 2.3 %copy.8 = bf16[128,4096]{1,0:T(8,128)(2,1)} copy(bf16[128,4096]{1,0:T(8,128)(2,1)} %get-tuple-element.4) | data formatting | bytes 2097152
  40.3 0.0 copy-done
  40.3 0.7 %copy.9 = f32[128,512]{1,0:T(8,128)} copy(f32[128,512]{1,0:T(8,128)S(1)} %copy-done) | data formatting | bytes 524288
Async XLA Ops:
  38.0 2.3 %copy-start = (f32[128,512]{1,0:T(8,128)S(1)}, f32[128,512]{1,0:T(8,128)}, u32[]{:S(2)}) copy-start(f32[128,512]{1,0:T(8,128)} %get-tuple-element.5) | copy-start | bytes 786436

commit v2 on v1

v2 whole, which is shorter than its diff:
```python
import functools
import math

import jax
import jax.numpy as jnp
from jax import lax
from jax.experimental import pallas as pl
from jax.experimental.pallas import tpu as pltpu
from jax.sharding import PartitionSpec as P

MESH = pl.DeviceIdType.MESH


def flip(index, mask, extent):
    out = 0
    bit = 1
    while bit < extent:
        digit = lax.rem(index // bit, 2)
        out = out + bit * (1 - digit if mask & bit else digit)
        bit *= 2
    return out


def lane_scale(scale_row, half):
    pick = (
        lax.broadcasted_iota(jnp.int32, (half // 2, half), 1) // 2
        == lax.broadcasted_iota(jnp.int32, (half // 2, half), 0)
    ).astype(jnp.float32).astype(jnp.bfloat16)
    rest = jnp.broadcast_to(scale_row, (16, half // 2))
    total = jnp.zeros((16, half), jnp.float32)
    for _ in range(3):
        top = rest.astype(jnp.bfloat16)
        total = total + jnp.dot(top, pick, preferred_element_type=jnp.float32)
        rest = rest - top.astype(jnp.float32)
    return total[0:1]


def kernel(
    ni, nj, acts, go, codes, scales, gin, gw,
    go_all, acts_v, codes_v, scale_v, scale_d, code_b, code_d, ac, pieces, part, rs,
    load_sem, go_send, go_recv, gh_send, gh_recv, fw_send, a_send, a_recv, p_send, p_recv,
    r_send, r_recv, s_sem, w_sem, up_send, down_send, w_recv,
):
    tok, width = acts.shape
    rows = codes.shape[0]
    half = rows // 2
    nz = nj // 2
    blk = rows // nj
    quarter = half // nz
    i = lax.axis_index("intra")
    j = lax.axis_index("inter")
    z = j // 2
    c = lax.rem(j, 2)
    oc = 1 - c
    me = 2 * i + c
    peers = {d: flip(i, d, ni) for d in range(ni)}
    near, diag = (1, 2), 3
    cores = (c, oc)

    def dev(ii, zz, cc):
        return {"intra": ii, "inter": 2 * zz + cc}

    def rdma(src, dst, s, r, where):
        return pltpu.make_async_remote_copy(
            src_ref=src, dst_ref=dst, send_sem=s, recv_sem=r, device_id=where, device_id_type=MESH
        )

    def arrived(ref, s, r):
        rdma(ref, ref, s, r, dev(i, z, oc)).wait_recv()

    sends = []

    def send(*args):
        cp = rdma(*args)
        cp.start()
        sends.append(cp)

    def go_slot(m):
        return go_all.at[pl.ds(pl.multiple_of(m * tok, tok), tok)]

    def go_half(m, n):
        return go_all.at[pl.ds(pl.multiple_of(m * tok + n * (tok // 2), tok // 2), tok // 2)]

    def ac_slot(h, m):
        return ac.at[h, pl.ds(pl.multiple_of(m * tok, tok), tok)]

    def cols_of(ii, cc):
        return pl.ds(pl.multiple_of(ii * rows + cc * half, half), half)

    half_start = pl.multiple_of(c * half, half)
    sc_start = pl.multiple_of(c * (half // 2), half // 2)
    load_codes = pltpu.make_async_copy(codes.at[pl.ds(half_start, half)], codes_v, load_sem.at[2])
    load_codes.start()
    load_scale = pltpu.make_async_copy(scales.at[:, pl.ds(sc_start, half // 2)], scale_v, load_sem.at[3])
    load_scale.start()
    load_go = pltpu.make_async_copy(go, go_slot(me), load_sem.at[0])
    load_go.start()
    load_acts = pltpu.make_async_copy(acts, acts_v, load_sem.at[1])
    load_acts.start()

    barrier = pltpu.get_barrier_semaphore()
    count = 0
    for d in range(ni):
        for k, cc in enumerate(cores):
            if d or k:
                pl.semaphore_signal(barrier, inc=1, device_id=dev(peers[d], z, cc), device_id_type=MESH)
                count += 1
    for k in range(1, nz):
        pl.semaphore_signal(barrier, inc=1, device_id=dev(i, lax.rem(z + k, nz), c), device_id_type=MESH)
        count += 1

    load_codes.wait()
    code_b[...] = codes_v[...].astype(jnp.float32).astype(jnp.bfloat16)
    load_go.wait()
    load_scale.wait()
    pl.semaphore_wait(barrier, count)

    for d in near:
        send(go_slot(me), go_slot(me), go_send.at[d], go_recv.at[me], dev(peers[d], z, c))
    send(go_slot(me), go_slot(me), go_send.at[0], go_recv.at[me], dev(i, z, oc))

    def slice_of(ref, q):
        return ref.at[pl.ds(pl.multiple_of(q * quarter, quarter), quarter)]

    send(slice_of(code_b, z), slice_of(code_d, z), w_sem.at[0], w_recv.at[z], dev(peers[diag], z, c))
    send(scale_v, scale_d, s_sem.at[0], s_sem.at[1], dev(peers[diag], z, c))

    load_acts.wait()
    order = [lax.rem(z + k, nz) for k in range(1, nz)] + [z]
    own = []

    def send_columns(h):
        for d in (diag,) + near + (0,):
            for k, cc in enumerate(cores):
                ii = peers[d]
                col = pl.multiple_of(ii * rows + (2 * h + cc) * blk, blk)
                src = acts_v.at[:, pl.ds(col, blk)]
                if d or k:
                    m = 2 * ii + cc
                    send(src, ac_slot(h, me), a_send.at[m, h], a_recv.at[me, h], dev(ii, z, cc))
                else:
                    cp = pltpu.make_async_copy(src, ac_slot(h, me), a_recv.at[me, h])
                    cp.start()
                    own.append(cp)

    send_columns(order[0])
    row_scale = lane_scale(scale_v[...], half)

    def wait_go(m):
        arrived(go_slot(m), go_send.at[0], go_recv.at[m])

    for n, d in enumerate(near):
        m = 2 * peers[d] + c
        wait_go(m)
        send(go_half(m, n), go_half(m, n), gh_send.at[n], gh_recv.at[n], dev(peers[diag ^ d], z, c))
        send(go_slot(m), go_slot(m), fw_send.at[d], go_recv.at[m], dev(i, z, oc))
    for h in order[1:]:
        send_columns(h)

    def pass_on(q, up):
        where = z + 1 if up else z - 1
        sem = up_send if up else down_send
        return rdma(slice_of(code_d, q), slice_of(code_d, q), sem.at[q], w_recv.at[q], dev(i, where, c))

    def may_pass(up):
        return z + 1 < nz if up else z >= 1

    def has(step, up):
        return z - step >= 0 if up else z + step < nz

    arrived(slice_of(code_d, z), w_sem.at[0], w_recv.at[z])
    for up in (True, False):
        @pl.when(may_pass(up))
        def _():
            pass_on(z, up).start()

    def relay(step):
        for up in (True, False):
            @pl.when(has(step, up))
            def _():
                q = z - step if up else z + step
                arrived(slice_of(code_d, q), w_sem.at[0], w_recv.at[q])

                @pl.when(may_pass(up))
                def _():
                    pass_on(q, up).start()

    def pieces_of(ii, code, scale):
        pair = go_all[pl.ds(pl.multiple_of(2 * ii * tok, 2 * tok), 2 * tok)]
        out = lax.dot_general(
            pair, code[...], (((1,), (1,)), ((), ())), preferred_element_type=jnp.float32
        )
        return (out * scale).astype(jnp.bfloat16)

    def piece(n, cc):
        return pieces.at[n, pl.ds(pl.multiple_of(cc * tok, tok), tok)]

    for d in near:
        ii = peers[d]
        wait_go(2 * ii + oc)
        pieces[d] = pieces_of(ii, code_b, row_scale)
        for cc in cores:
            m = 2 * ii + cc
            send(piece(d, cc), gin.at[:, cols_of(i, c)], p_send.at[m], p_recv.at[me], dev(ii, z, cc))
    wait_go(2 * i + oc)
    pieces[0] = pieces_of(i, code_b, row_scale)
    send(piece(0, oc), gin.at[:, cols_of(i, c)], p_send.at[2 * i + oc], p_recv.at[me], dev(i, z, oc))
    keep = pltpu.make_async_copy(piece(0, c), gin.at[:, cols_of(i, c)], p_recv.at[me])
    keep.start()

    m = 2 * peers[diag] + c
    for n in range(2):
        arrived(go_half(m, n), gh_send.at[n], gh_recv.at[n])
    send(go_slot(m), go_slot(m), fw_send.at[diag], go_recv.at[m], dev(i, z, oc))
    wait_go(2 * peers[diag] + oc)

    mine = None
    for n, h in enumerate(order):
        own[n].wait()
        for d in range(ni):
            for k, cc in enumerate(cores):
                if d or k:
                    m = 2 * peers[d] + cc
                    arrived(ac_slot(h, m), a_send.at[m, h], a_recv.at[m, h])
        term = lax.dot_general(
            ac[h], go_all[...], (((0,), (0,)), ((), ())), preferred_element_type=jnp.float32
        )
        if n < nz - 1:
            part[n] = term.astype(jnp.bfloat16)
            send(part.at[n], rs.at[z], r_send.at[n], r_recv.at[z], dev(i, h, c))
            relay(n + 1)
        else:
            mine = term

    arrived(scale_d, s_sem.at[0], s_sem.at[1])
    dd = peers[diag]
    pieces[diag] = pieces_of(i, code_d, lane_scale(scale_d[...], half))
    send(piece(diag, oc), gin.at[:, cols_of(dd, c)], p_send.at[2 * dd + c], p_recv.at[2 * dd + c], dev(i, z, oc))
    keep_d = pltpu.make_async_copy(piece(diag, c), gin.at[:, cols_of(dd, c)], load_sem.at[4])
    keep_d.start()

    for k in range(1, nz):
        h = lax.rem(z + k, nz)
        arrived(rs.at[h], r_send.at[0], r_recv.at[h])
        mine = mine + rs[h].astype(jnp.float32)
    gw[...] = mine * (1.0 / math.sqrt(tok * ni * nj))

    keep.wait()
    keep_d.wait()
    for d in range(ni):
        for k, cc in enumerate(cores):
            if (d != diag and (d or k)) or (d == diag and k):
                ii = peers[d]
                block = gin.at[:, cols_of(ii, cc)]
                arrived(block, p_send.at[2 * ii + cc], p_recv.at[2 * ii + cc])
    for cp in sends:
        cp.wait_send()
    for step in range(nz):
        for up in (True, False):
            @pl.when(jnp.logical_and(has(step, up), may_pass(up)))
            def _():
                pass_on(z - step if up else z + step, up).wait_send()


def fused(ni, nj, acts, grad_out, codes, scales):
    tok, width = acts.shape
    kv = grad_out.shape[1]
    rows = codes.shape[0]
    half, nz, blk = rows // 2, nj // 2, rows // nj
    group = 2 * ni
    dma = pltpu.SemaphoreType.DMA
    bf16 = jnp.bfloat16
    anyspace = pl.BlockSpec(memory_space=pl.ANY)
    return tuple(pl.pallas_call(
        functools.partial(kernel, ni, nj),
        out_shape=(
            pltpu.VMEM((tok, width), bf16),
            pltpu.VMEM((blk, kv), jnp.float32),
        ),
        in_specs=[anyspace] * 4,
        out_specs=(pl.BlockSpec(memory_space=pltpu.VMEM),) * 2,
        scratch_shapes=[
            pltpu.VMEM((group * tok, kv), bf16),
            pltpu.VMEM((tok, width), bf16),
            pltpu.VMEM((half, kv), jnp.int32),
            pltpu.VMEM((1, half // 2), jnp.float32),
            pltpu.VMEM((1, half // 2), jnp.float32),
            pltpu.VMEM((half, kv), bf16),
            pltpu.VMEM((half, kv), bf16),
            pltpu.VMEM((nz, group * tok, blk), bf16),
            pltpu.VMEM((ni, 2 * tok, half), bf16),
            pltpu.VMEM((max(nz - 1, 1), blk, kv), bf16),
            pltpu.VMEM((nz, blk, kv), bf16),
            dma((5,)),
            dma((ni,)), dma((group,)), dma((2,)), dma((2,)), dma((ni,)),
            dma((group, nz)), dma((group, nz)),
            dma((group,)), dma((group,)),
            dma((nz,)), dma((nz,)),
            dma((2,)), dma((1,)), dma((nz,)), dma((nz,)), dma((nz,)),
        ],
        compiler_params=pltpu.CompilerParams(collective_id=0, has_side_effects=True),
    )(acts, grad_out, codes, scales.reshape(1, -1)))


def plain(acts, grad_out, codes, scales):
    rows = codes.shape[0]
    width_kv = codes.shape[1]
    blocks = codes.astype(jnp.float32).reshape(rows // 2, 2 * width_kv) * scales[:, None]
    local_weight = blocks.reshape(rows, width_kv).astype(jnp.bfloat16)
    n_group = lax.axis_size("intra")
    n_cross = lax.axis_size("inter")
    factor = 1.0 / math.sqrt(acts.shape[0] * n_group * n_cross)
    contract = (((0,), (0,)), ((), ()))
    group_cot = lax.all_gather(grad_out, "intra", axis=0, tiled=True)
    columns_owned = lax.all_to_all(acts, "intra", split_axis=1, concat_axis=0, tiled=True)
    grad_w = lax.psum_scatter(
        lax.dot_general(columns_owned, group_cot, contract, preferred_element_type=jnp.float32)
        * factor,
        "inter",
        scatter_dimension=0,
        tiled=True,
    )
    pieces = jnp.dot(group_cot, local_weight.T, preferred_element_type=jnp.float32).astype(
        jnp.bfloat16
    )
    grad_in = lax.all_to_all(pieces, "intra", split_axis=0, concat_axis=1, tiled=True)
    return (grad_in, grad_w)


def solution(mesh):
    ni, nj = mesh.shape["intra"], mesh.shape["inter"]

    def per_device(acts, grad_out, codes, scales):
        rows = codes.shape[0]
        aligned = rows % (nj * 128) == 0 and rows % 512 == 0 and acts.shape[0] % 16 == 0
        if aligned and nj % 2 == 0 and ni == 4 and acts.shape[1] == ni * rows:
            return fused(ni, nj, acts, grad_out, codes, scales)
        return plain(acts, grad_out, codes, scales)

    in_specs = (
        P(("intra", "inter"), None),
        P(("intra", "inter"), None),
        P("intra", None),
        P("intra"),
    )
    out_specs = (P(("intra", "inter"), None), P(("intra", "inter"), None))
    return jax.shard_map(
        per_device, mesh=mesh, in_specs=in_specs, out_specs=out_specs, check_vma=False
    )
```

time: 41.2 us -> 42.8 us (1.039)
  Pallas kernels: 37.4 us -> 39.9 us
  local copies, waits for them, and re-layouts: 3.04 us -> 1.67 us
    pallas_call x1, Pallas kernels: 37.4 us -> 39.9 us  [fused(): pl.pallas_call(functools.partial(kernel, ni, nj), out_shape=(pltpu.VMEM((...]
    unnamed x4 -> x2, local copies, waits for them, and re-layouts: 3.04 us -> 1.67 us
where the time goes in v2:
time: 42.8 us; the launch traced here: 42.2 us
  Pallas kernels  39.9 us (93%)
  local copies, waits for them, and re-layouts  1.67 us (4%)
  between operations  0.64 us (1%)
    pallas_call x1, Pallas kernels, fused(): pl.pallas_call(functools.partial(kernel, ni, nj), out_shape=(pltpu.VMEM((...  39.9 us
    unnamed x2, local copies, waits for them, and re-layouts  1.67 us

profile of v2, /device:TPU:1, one launch (start us, length us, event | category | flops | bytes accessed | tf_op | source)
XLA Modules:
  0.0 42.2 jit_solution(15242103711669351790)
XLA Ops:
  0.6 39.9 %shard_map.59 = (bf16[128,4096]{1,0:T(8,128)(2,1)S(1)}, f32[128,512]{1,0:T(8,128)S(1)}) custom-call(bf16[128,4096]{1,0:T(8,128)(2,1)} %acts.1, bf16[128,512]{1,0:T(8,128)(2,1)} %go.1, s32[1024,512]{1,0:T(8,128)} %codes.1, f32[1,512]{1,0:T(1,128)} %bitcast.1), custom_call_target="tpu_custom_call" | custom-call | tf_op jit(solution)/shard_map/pallas_call | solution.py:274
  40.6 1.0 %copy.8 = bf16[128,4096]{1,0:T(8,128)(2,1)} copy(bf16[128,4096]{1,0:T(8,128)(2,1)S(1)} %get-tuple-element.2) | data formatting | bytes 2097152
  41.5 0.7 %copy.9 = f32[128,512]{1,0:T(8,128)} copy(f32[128,512]{1,0:T(8,128)S(1)} %get-tuple-element.3) | data formatting | bytes 524288

commit v3 on v2

--- a/solution.py
+++ b/solution.py
@@ -37,16 +37,15 @@
 
 def kernel(
     ni, nj, acts, go, codes, scales, gin, gw,
-    go_all, acts_v, codes_v, scale_v, scale_d, code_b, code_d, ac, pieces, part, rs,
+    go_all, acts_v, codes_v, scale_v, code_b, ac, pieces, part, rs,
     load_sem, go_send, go_recv, gh_send, gh_recv, fw_send, a_send, a_recv, p_send, p_recv,
-    r_send, r_recv, s_sem, w_sem, up_send, down_send, w_recv,
+    r_send, r_recv,
 ):
     tok, width = acts.shape
     rows = codes.shape[0]
     half = rows // 2
     nz = nj // 2
     blk = rows // nj
-    quarter = half // nz
     i = lax.axis_index("intra")
     j = lax.axis_index("inter")
     z = j // 2
@@ -118,12 +117,6 @@
     for d in near:
         send(go_slot(me), go_slot(me), go_send.at[d], go_recv.at[me], dev(peers[d], z, c))
     send(go_slot(me), go_slot(me), go_send.at[0], go_recv.at[me], dev(i, z, oc))
-
-    def slice_of(ref, q):
-        return ref.at[pl.ds(pl.multiple_of(q * quarter, quarter), quarter)]
-
-    send(slice_of(code_b, z), slice_of(code_d, z), w_sem.at[0], w_recv.at[z], dev(peers[diag], z, c))
-    send(scale_v, scale_d, s_sem.at[0], s_sem.at[1], dev(peers[diag], z, c))
 
     load_acts.wait()
     order = [lax.rem(z + k, nz) for k in range(1, nz)] + [z]
@@ -157,34 +150,6 @@
     for h in order[1:]:
         send_columns(h)
 
-    def pass_on(q, up):
-        where = z + 1 if up else z - 1
-        sem = up_send if up else down_send
-        return rdma(slice_of(code_d, q), slice_of(code_d, q), sem.at[q], w_recv.at[q], dev(i, where, c))
-
-    def may_pass(up):
-        return z + 1 < nz if up else z >= 1
-
-    def has(step, up):
-        return z - step >= 0 if up else z + step < nz
-
-    arrived(slice_of(code_d, z), w_sem.at[0], w_recv.at[z])
-    for up in (True, False):
-        @pl.when(may_pass(up))
-        def _():
-            pass_on(z, up).start()
-
-    def relay(step):
-        for up in (True, False):
-            @pl.when(has(step, up))
-            def _():
-                q = z - step if up else z + step
-                arrived(slice_of(code_d, q), w_sem.at[0], w_recv.at[q])
-
-                @pl.when(may_pass(up))
-                def _():
-                    pass_on(q, up).start()
-
     def pieces_of(ii, code, scale):
         pair = go_all[pl.ds(pl.multiple_of(2 * ii * tok, 2 * tok), 2 * tok)]
         out = lax.dot_general(
@@ -213,6 +178,11 @@
         arrived(go_half(m, n), gh_send.at[n], gh_recv.at[n])
     send(go_slot(m), go_slot(m), fw_send.at[diag], go_recv.at[m], dev(i, z, oc))
     wait_go(2 * peers[diag] + oc)
+    dd = peers[diag]
+    pieces[diag] = pieces_of(dd, code_b, row_scale)
+    for cc in cores:
+        m = 2 * dd + cc
+        send(piece(diag, cc), gin.at[:, cols_of(i, c)], p_send.at[m], p_recv.at[me], dev(dd, z, cc))
 
     mine = None
     for n, h in enumerate(order):
@@ -228,16 +198,8 @@
         if n < nz - 1:
             part[n] = term.astype(jnp.bfloat16)
             send(part.at[n], rs.at[z], r_send.at[n], r_recv.at[z], dev(i, h, c))
-            relay(n + 1)
         else:
             mine = term
-
-    arrived(scale_d, s_sem.at[0], s_sem.at[1])
-    dd = peers[diag]
-    pieces[diag] = pieces_of(i, code_d, lane_scale(scale_d[...], half))
-    send(piece(diag, oc), gin.at[:, cols_of(dd, c)], p_send.at[2 * dd + c], p_recv.at[2 * dd + c], dev(i, z, oc))
-    keep_d = pltpu.make_async_copy(piece(diag, c), gin.at[:, cols_of(dd, c)], load_sem.at[4])
-    keep_d.start()
 
     for k in range(1, nz):
         h = lax.rem(z + k, nz)
@@ -246,20 +208,14 @@
     gw[...] = mine * (1.0 / math.sqrt(tok * ni * nj))
 
     keep.wait()
-    keep_d.wait()
     for d in range(ni):
         for k, cc in enumerate(cores):
-            if (d != diag and (d or k)) or (d == diag and k):
+            if d or k:
                 ii = peers[d]
                 block = gin.at[:, cols_of(ii, cc)]
                 arrived(block, p_send.at[2 * ii + cc], p_recv.at[2 * ii + cc])
     for cp in sends:
         cp.wait_send()
-    for step in range(nz):
-        for up in (True, False):
-            @pl.when(jnp.logical_and(has(step, up), may_pass(up)))
-            def _():
-                pass_on(z - step if up else z + step, up).wait_send()
 
 
 def fused(ni, nj, acts, grad_out, codes, scales):
@@ -284,19 +240,16 @@
             pltpu.VMEM((tok, width), bf16),
             pltpu.VMEM((half, kv), jnp.int32),
             pltpu.VMEM((1, half // 2), jnp.float32),
-            pltpu.VMEM((1, half // 2), jnp.float32),
-            pltpu.VMEM((half, kv), bf16),
             pltpu.VMEM((half, kv), bf16),
             pltpu.VMEM((nz, group * tok, blk), bf16),
             pltpu.VMEM((ni, 2 * tok, half), bf16),
             pltpu.VMEM((max(nz - 1, 1), blk, kv), bf16),
             pltpu.VMEM((nz, blk, kv), bf16),
-            dma((5,)),
+            dma((4,)),
             dma((ni,)), dma((group,)), dma((2,)), dma((2,)), dma((ni,)),
             dma((group, nz)), dma((group, nz)),
             dma((group,)), dma((group,)),
             dma((nz,)), dma((nz,)),
-            dma((2,)), dma((1,)), dma((nz,)), dma((nz,)), dma((nz,)),
         ],
         compiler_params=pltpu.CompilerParams(collective_id=0, has_side_effects=True),
     )(acts, grad_out, codes, scales.reshape(1, -1)))

time: 42.8 us -> 37.6 us (0.88)
  Pallas kernels: 39.9 us -> 35.1 us
    pallas_call x1, Pallas kernels: 39.9 us -> 35.1 us  [fused(): pl.pallas_call(functools.partial(kernel, ni, nj), out_shape=(pltpu.VMEM((...]
where the time goes in v3:
time: 37.6 us; the launch traced here: 37.4 us
  Pallas kernels  35.1 us (93%)
  local copies, waits for them, and re-layouts  1.67 us (4%)
  between operations  0.64 us (2%)
    pallas_call x1, Pallas kernels, fused(): pl.pallas_call(functools.partial(kernel, ni, nj), out_shape=(pltpu.VMEM((...  35.1 us
    unnamed x2, local copies, waits for them, and re-layouts  1.67 us

profile of v3, /device:TPU:1, one launch (start us, length us, event | category | flops | bytes accessed | tf_op | source)
XLA Modules:
  0.0 37.4 jit_solution(9473942619301385678)
XLA Ops:
  0.6 35.1 %shard_map.59 = (bf16[128,4096]{1,0:T(8,128)(2,1)S(1)}, f32[128,512]{1,0:T(8,128)S(1)}) custom-call(bf16[128,4096]{1,0:T(8,128)(2,1)} %acts.1, bf16[128,512]{1,0:T(8,128)(2,1)} %go.1, s32[1024,512]{1,0:T(8,128)} %codes.1, f32[1,512]{1,0:T(1,128)} %bitcast.1), custom_call_target="tpu_custom_call" | custom-call | tf_op jit(solution)/shard_map/pallas_call | solution.py:230
  35.8 1.0 %copy.8 = bf16[128,4096]{1,0:T(8,128)(2,1)} copy(bf16[128,4096]{1,0:T(8,128)(2,1)S(1)} %get-tuple-element.2) | data formatting | bytes 2097152
  36.7 0.7 %copy.9 = f32[128,512]{1,0:T(8,128)} copy(f32[128,512]{1,0:T(8,128)S(1)} %get-tuple-element.3) | data formatting | bytes 524288

commit v4 on v3

--- a/solution.py
+++ b/solution.py
@@ -88,15 +88,15 @@
 
     half_start = pl.multiple_of(c * half, half)
     sc_start = pl.multiple_of(c * (half // 2), half // 2)
+    load_go = pltpu.make_async_copy(go, go_slot(me), load_sem.at[0])
+    load_go.start()
+    load_acts = pltpu.make_async_copy(acts, acts_v, load_sem.at[1])
+    load_acts.start()
+
     load_codes = pltpu.make_async_copy(codes.at[pl.ds(half_start, half)], codes_v, load_sem.at[2])
     load_codes.start()
     load_scale = pltpu.make_async_copy(scales.at[:, pl.ds(sc_start, half // 2)], scale_v, load_sem.at[3])
     load_scale.start()
-    load_go = pltpu.make_async_copy(go, go_slot(me), load_sem.at[0])
-    load_go.start()
-    load_acts = pltpu.make_async_copy(acts, acts_v, load_sem.at[1])
-    load_acts.start()
-
     barrier = pltpu.get_barrier_semaphore()
     count = 0
     for d in range(ni):
@@ -108,10 +108,7 @@
         pl.semaphore_signal(barrier, inc=1, device_id=dev(i, lax.rem(z + k, nz), c), device_id_type=MESH)
         count += 1
 
-    load_codes.wait()
-    code_b[...] = codes_v[...].astype(jnp.float32).astype(jnp.bfloat16)
     load_go.wait()
-    load_scale.wait()
     pl.semaphore_wait(barrier, count)
 
     for d in near:
@@ -123,7 +120,7 @@
     own = []
 
     def send_columns(h):
-        for d in (diag,) + near + (0,):
+        for d in near + (0, diag):
             for k, cc in enumerate(cores):
                 ii = peers[d]
                 col = pl.multiple_of(ii * rows + (2 * h + cc) * blk, blk)
@@ -137,6 +134,9 @@
                     own.append(cp)
 
     send_columns(order[0])
+    load_codes.wait()
+    code_b[...] = codes_v[...].astype(jnp.float32).astype(jnp.bfloat16)
+    load_scale.wait()
     row_scale = lane_scale(scale_v[...], half)
 
     def wait_go(m):

time: 37.6 us -> 37.6 us (level)
  no operation moved by 1% of the time
where the time goes in v4:
time: 37.6 us; the launch traced here: 37.4 us
  Pallas kernels  35.1 us (93%)
  local copies, waits for them, and re-layouts  1.67 us (4%)
  between operations  0.64 us (2%)
    pallas_call x1, Pallas kernels, fused(): pl.pallas_call(functools.partial(kernel, ni, nj), out_shape=(pltpu.VMEM((...  35.1 us
    unnamed x2, local copies, waits for them, and re-layouts  1.67 us

profile of v4, /device:TPU:1, one launch (start us, length us, event | category | flops | bytes accessed | tf_op | source)
XLA Modules:
  0.0 37.4 jit_solution(17246262183885056466)
XLA Ops:
  0.6 35.1 %shard_map.59 = (bf16[128,4096]{1,0:T(8,128)(2,1)S(1)}, f32[128,512]{1,0:T(8,128)S(1)}) custom-call(bf16[128,4096]{1,0:T(8,128)(2,1)} %acts.1, bf16[128,512]{1,0:T(8,128)(2,1)} %go.1, s32[1024,512]{1,0:T(8,128)} %codes.1, f32[1,512]{1,0:T(1,128)} %bitcast.1), custom_call_target="tpu_custom_call" | custom-call | tf_op jit(solution)/shard_map/pallas_call | solution.py:230
  35.8 1.0 %copy.8 = bf16[128,4096]{1,0:T(8,128)(2,1)} copy(bf16[128,4096]{1,0:T(8,128)(2,1)S(1)} %get-tuple-element.2) | data formatting | bytes 2097152
  36.7 0.7 %copy.9 = f32[128,512]{1,0:T(8,128)} copy(f32[128,512]{1,0:T(8,128)S(1)} %get-tuple-element.3) | data formatting | bytes 524288
